TPU v7x, 128 devices: a whole 4x4x4 slice. The times are simulated.
128 devices in a mesh: depth: 16 (over y, x), screen: 8 (over z, core).
Axes of the slice: x: 4, y: 4, z: 4, core: 2. Of those that a mesh axis runs over, the one named last changes fastest.
Arguments:
- block_tile: int32 [16, 16384], P('depth', 'screen'), may hold values from 0 to 511
- block_count: int32 [16, 8], P('depth', 'screen'), may hold values from 256 to 2048, as said below
- slab_rank: int32 [16], replicated, may hold values from 0 to 15, each once
- corner: int32 [2, 16, 16384, 128], P(None, 'depth', 'screen'), may hold values from 0 to 16
- offset: float32 [2, 16, 16384, 128], P(None, 'depth', 'screen'), may hold values from 0.25 to 0.75
- radius: float32 [16, 16384, 128], P('depth', 'screen'), may hold values from 3 to 8
- emission: float32 [3, 16, 16384, 128], P(None, 'depth', 'screen'), may hold values from 0.002 to 0.02
- extinction: float32 [16, 16384, 128], P('depth', 'screen'), may hold values from 0.001 to 0.01
Outputs:
- image_tiles: float32 [512, 32, 128], P(('depth', 'screen'))
Inputs may be any that keep to these rules, and one draw needn't show every extreme that they name: The live slots of a device are its first block_count slots; one device of every draw has all 2048 slots live. `block_tile`: a block holds particles of one tile. `corner`: a footprint box lies inside its tile. `slab_rank`: each slab once.
All inputs are finite; a program needn't handle non-finite values.
Results may differ from a plain program's by a relative error of at most 0.0003.
Values sent between devices are 32-bit elements; how exact they have to be, the bound alone decides.
A program may use at most 128 MiB of HBM per device.

v0:
```python
import jax
import jax.numpy as jnp
from jax import lax
from jax.sharding import Mesh
from jax.sharding import PartitionSpec as P

TS = 32
FOOT = 16
TILE_DEV = 4
SCREEN = ("screen_0", "screen_1")
DEPTH_SCREEN = ("depth", "screen_0", "screen_1")


def sum_in_order(pieces, axes, turns):
    inside = pieces.shape[1:]
    pieces = pieces.reshape(*(lax.axis_size(a) for a in axes), *inside)
    pieces = jnp.moveaxis(pieces, turns, range(len(axes))).reshape(-1, *inside)
    for k in turns:
        pieces = lax.psum_scatter(pieces, axes[k], scatter_dimension=0, tiled=True)
    return pieces[0]


def cut_along(shard, dim, devices):
    before, after = (shard.shape[:dim], shard.shape[dim + 1 :])
    return jnp.moveaxis(shard.reshape(*before, devices, -1, *after), dim, 0)


def summed_rows(shard, axes, turns, dim):
    devices = lax.axis_size(axes)
    return sum_in_order(cut_along(shard, dim, devices), axes, turns)


def axis_weights(corner, offset, radius, tile_side, foot):
    pixel_index = jnp.arange(tile_side, dtype=jnp.int32)
    pixel_centre = pixel_index.astype(jnp.float32) + 0.5
    centres = corner.astype(jnp.float32) + foot * offset
    scaled = (pixel_centre - centres[..., None]) / radius[..., None]
    bump_shape = jnp.maximum(1.0 - scaled * scaled, 0.0)
    inside = (pixel_index >= corner[..., None]) & (pixel_index < corner[..., None] + foot)
    return jnp.where(inside, bump_shape * bump_shape, 0.0)


def deposit(corner, offset, radius, emission, extinction, block_live, tile_side, foot):
    across = axis_weights(corner[0], offset[0], radius, tile_side, foot)
    down_weights = axis_weights(corner[1], offset[1], radius, tile_side, foot)
    fields = jnp.concatenate([emission, extinction[None]], 0) * block_live[None, :, None]
    spread = fields[..., None] * across[None]
    deposit_out = jnp.einsum(
        "gpy,cgpx->gycx", down_weights, spread, precision=lax.Precision.HIGHEST
    )
    return deposit_out.reshape(deposit_out.shape[0], tile_side, 4 * tile_side)


def composite(stacked, slab_rank):
    slab_num, tile_num, tile_side, row_width = stacked.shape
    pieces = stacked.reshape(slab_num, tile_num, tile_side, 4, row_width // 4)
    glow_part = pieces[:, :, :, :3, :]
    optical = pieces[:, :, :, 3:, :]
    before = (slab_rank[None, :] < slab_rank[:, None]).astype(jnp.float32)
    prior_depth = jnp.einsum("jk,ktyax->jtyax", before, optical, precision=lax.Precision.HIGHEST)
    lighting = jnp.sum(jnp.exp(-prior_depth) * glow_part * jnp.exp(-0.5 * optical), axis=0)
    coverage = 1.0 - jnp.exp(-jnp.sum(optical, axis=0))
    return jnp.concatenate([lighting, coverage], axis=2).reshape(tile_num, tile_side, row_width)


def shards(block_tile, block_count, slab_rank, corner, offset, radius, emission, extinction):
    slots = block_tile.shape[1]
    group_size = min(256, slots)
    depth_size = lax.axis_size("depth")
    screen_size = lax.axis_size(SCREEN)
    tiles_all = TILE_DEV * depth_size * screen_size
    live_count = block_count[0, 0]
    rounds = (live_count + group_size - 1) // group_size

    def one_round(round_index, tile_sums):
        first_row = round_index * group_size
        ids_now = lax.dynamic_slice_in_dim(block_tile[0], first_row, group_size, 0)
        corner_now = lax.dynamic_slice_in_dim(corner[:, 0], first_row, group_size, 1)
        offset_now = lax.dynamic_slice_in_dim(offset[:, 0], first_row, group_size, 1)
        radius_now = lax.dynamic_slice_in_dim(radius[0], first_row, group_size, 0)
        glow_now = lax.dynamic_slice_in_dim(emission[:, 0], first_row, group_size, 1)
        rate_now = lax.dynamic_slice_in_dim(extinction[0], first_row, group_size, 0)
        live_now = (first_row + jnp.arange(group_size, dtype=jnp.int32) < live_count).astype(
            jnp.float32
        )
        deposit_out = deposit(
            corner_now, offset_now, radius_now, glow_now, rate_now, live_now, TS, FOOT
        )
        return tile_sums.at[ids_now].add(deposit_out)

    partial_value = lax.fori_loop(
        0, rounds, one_round, jnp.zeros((tiles_all, TS, 4 * TS), jnp.float32)
    )
    shaped = partial_value.reshape(depth_size, screen_size * TILE_DEV, TS, 4 * TS)
    owned = summed_rows(shaped, SCREEN, (1, 0), 1)
    return composite(
        lax.all_to_all(owned, "depth", split_axis=0, concat_axis=0, tiled=True), slab_rank
    )


def solution(mesh):
    torus = Mesh(mesh.devices.reshape(mesh.shape["depth"], 4, 2), ("depth", "screen_0", "screen_1"))
    placed = (
        P("depth", SCREEN),
        P("depth", SCREEN),
        P(),
        P(None, "depth", SCREEN, None),
        P(None, "depth", SCREEN, None),
        P("depth", SCREEN, None),
        P(None, "depth", SCREEN, None),
        P("depth", SCREEN, None),
    )
    return jax.shard_map(
        shards, mesh=torus, in_specs=placed, out_specs=P(DEPTH_SCREEN, None, None), check_vma=False
    )
```

profile of v0, /device:TPU:0, one launch (start us, length us, event | category | flops | bytes accessed | tf_op | source)
XLA Modules:
  0.0 1255.3 jit_solution(7698204150471641096)
XLA Ops:
  7.2 4.3 broadcast_in_dim.4
  11.5 422.2 %while.10 = (s32[]{:T(128)}, f32[512,32,128]{2,1,0:T(8,128)}, s32[]{:T(128)}, s32[1,2048]{1,0:T(1,128)}, s32[2,1,2048,128]{3,2,1,0:T(8,128)}, /*index=5*/f32[2,1...) while((s32[]{:T(128)}, f32[512,32,128]{2,1,0:T(8,128)}, ...), condition=%wide.region_2.3_spmd, body=%wide.region_0.2_spmd.sunk | while | flops 1637353088 | bytes 48240240 | solution.py:91
  14.5 1.8 multiply_select_fusion.2
  19.5 79.2 %fusion.46 = f32[256,32,4,32]{3,1,2,0:T(8,128)} fusion(f32[256,128,32]{1,2,0:T(8,128)S(1)} %multiply_select_fusion.2, f32[4,256,128]{2,0,1:T(4,128)S(1)} %maximum_multiply_fusion.2, f32[256,128]{1,0:T(8,128)S(1)} %dynamic-slice_bitcast_fusion.6, f32[256,128]{1,0:T(8,128)S(1)} %get-tuple-element.201, f32[32]{0:T(128)S(1)} %convert_add_fusion.2, ...), kind=kOutput, calls=%fused_computation.1.clone.1 | convolution fusion | flops 1625292800 | bytes 9437312 | tf_op jit(solution)/shard_map/while/body/gpy,cgpx->gycx/dot_general | solution.py:48
  98.8 13.3 %copy.51 = f32[256,32,4,32]{0,3,2,1:T(8,128)} copy(f32[256,32,4,32]{3,1,2,0:T(8,128)} %fusion.46) | data formatting | bytes 8388608 | tf_op jit(solution)/shard_map/while/body/gpy,cgpx->gycx/dot_general | solution.py:48
  112.1 5.5 copy.52
  118.3 34.0 %scatter_fusion = f32[512,32,128]{2,1,0:T(8,128)} fusion(f32[512,32,128]{2,1,0:T(8,128)} %get-tuple-element.219, s32[256]{0:T(256)S(1)} %bitcast.76, f32[256,32,128]{2,1,0:T(8,128)} %copy.52), kind=kCustom, calls=%fused_computation.clone.1 | custom fusion | flops 1048576 | bytes 12583936 | tf_op jit(solution)/shard_map/while/body/scatter-add | solution.py:89
  155.2 1.8 multiply_select_fusion.2
  160.3 79.2 %fusion.46 = f32[256,32,4,32]{3,1,2,0:T(8,128)} fusion(f32[256,128,32]{1,2,0:T(8,128)S(1)} %multiply_select_fusion.2, f32[4,256,128]{2,0,1:T(4,128)S(1)} %maximum_multiply_fusion.2, f32[256,128]{1,0:T(8,128)S(1)} %dynamic-slice_bitcast_fusion.6, f32[256,128]{1,0:T(8,128)S(1)} %get-tuple-element.201, f32[32]{0:T(128)S(1)} %convert_add_fusion.2, ...), kind=kOutput, calls=%fused_computation.1.clone.1 | convolution fusion | flops 1625292800 | bytes 9437312 | tf_op jit(solution)/shard_map/while/body/gpy,cgpx->gycx/dot_general | solution.py:48
  239.6 13.3 %copy.51 = f32[256,32,4,32]{0,3,2,1:T(8,128)} copy(f32[256,32,4,32]{3,1,2,0:T(8,128)} %fusion.46) | data formatting | bytes 8388608 | tf_op jit(solution)/shard_map/while/body/gpy,cgpx->gycx/dot_general | solution.py:48
  252.9 5.5 copy.52
  259.0 34.0 %scatter_fusion = f32[512,32,128]{2,1,0:T(8,128)} fusion(f32[512,32,128]{2,1,0:T(8,128)} %get-tuple-element.219, s32[256]{0:T(256)S(1)} %bitcast.76, f32[256,32,128]{2,1,0:T(8,128)} %copy.52), kind=kCustom, calls=%fused_computation.clone.1 | custom fusion | flops 1048576 | bytes 12583936 | tf_op jit(solution)/shard_map/while/body/scatter-add | solution.py:89
  296.0 1.8 multiply_select_fusion.2
  301.0 79.2 %fusion.46 = f32[256,32,4,32]{3,1,2,0:T(8,128)} fusion(f32[256,128,32]{1,2,0:T(8,128)S(1)} %multiply_select_fusion.2, f32[4,256,128]{2,0,1:T(4,128)S(1)} %maximum_multiply_fusion.2, f32[256,128]{1,0:T(8,128)S(1)} %dynamic-slice_bitcast_fusion.6, f32[256,128]{1,0:T(8,128)S(1)} %get-tuple-element.201, f32[32]{0:T(128)S(1)} %convert_add_fusion.2, ...), kind=kOutput, calls=%fused_computation.1.clone.1 | convolution fusion | flops 1625292800 | bytes 9437312 | tf_op jit(solution)/shard_map/while/body/gpy,cgpx->gycx/dot_general | solution.py:48
  380.3 13.3 %copy.51 = f32[256,32,4,32]{0,3,2,1:T(8,128)} copy(f32[256,32,4,32]{3,1,2,0:T(8,128)} %fusion.46) | data formatting | bytes 8388608 | tf_op jit(solution)/shard_map/while/body/gpy,cgpx->gycx/dot_general | solution.py:48
  393.6 5.5 copy.52
  399.8 33.9 %scatter_fusion = f32[512,32,128]{2,1,0:T(8,128)} fusion(f32[512,32,128]{2,1,0:T(8,128)} %get-tuple-element.219, s32[256]{0:T(256)S(1)} %bitcast.76, f32[256,32,128]{2,1,0:T(8,128)} %copy.52), kind=kCustom, calls=%fused_computation.clone.1 | custom fusion | flops 1048576 | bytes 12583936 | tf_op jit(solution)/shard_map/while/body/scatter-add | solution.py:89
  433.7 8.5 copy.30
  442.3 718.1 %reduce-scatter.3.cloned.1.call-done = f32[4,16,4,32,128]{4,3,2,1,0:T(8,128)} async-done(((f32[8,16,4,32,128]{4,3,2,1,0:T(8,128)}), f32[4,16,4,32,128]{4,3,2,1,0:T(8,128)}) %reduce-scatter.3.cloned.1.call-update) | async-done | bytes 4194320 | tf_op jit(solution)/shard_map/reduce_scatter | solution.py:19
  1160.4 50.8 %reduce-scatter.5.cloned.1.call-done = f32[1,16,4,32,128]{4,3,2,1,0:T(8,128)} async-done(((f32[4,16,4,32,128]{4,3,2,1,0:T(8,128)}), f32[1,16,4,32,128]{4,3,2,1,0:T(8,128)}) %reduce-scatter.5.cloned.1.call-update) | async-done | bytes 1048592 | tf_op jit(solution)/shard_map/reduce_scatter | solution.py:19
  1211.2 23.9 %all_to_all.5 = f32[16,4,32,128]{3,2,1,0:T(8,128)S(1)} all-to-all(f32[16,4,32,128]{3,2,1,0:T(8,128)} %bitcast.73), channel_id=1, replica_groups=mesh['depth'=16,'screen_0'=4,'screen_1'=2] {'depth'}, dimensions={0} | all-to-all | bytes 2097152 | tf_op jit(solution)/shard_map/all_to_all | solution.py:97
  1235.2 3.1 reshape.177
  1238.3 3.9 fusion.38
  1244.9 2.6 fusion.30
  (45 shorter events, 24.2 us)
Async XLA Ops:
  6.5 1153.8 %reduce-scatter.3.cloned.1.call-start = ((), (), s32[]{:S(2)}) async-start(), calls=%async_computation.3 | async-start | bytes 12582912 | tf_op jit(solution)/shard_map/reduce_scatter | solution.py:19
  442.2 769.0 %reduce-scatter.5.cloned.1.call-start = ((), (), s32[]{:S(2)}) async-start(), calls=%async_computation.4 | async-start | bytes 5242880 | tf_op jit(solution)/shard_map/reduce_scatter | solution.py:19
  1235.2 7.8 copy-start.1
  1242.2 2.7 copy-start
Sparse Core Ops, SparseCore 0:
  442.3 717.9 reduce-scatter.2
  1162.8 48.4 reduce-scatter.4
where the time goes:
time: 1260 us
  waiting for transfers between devices  769 us (61%)
  matrix products  239 us (19%)
  other arithmetic  126 us (10%)
  local copies, waits for them, and re-layouts  83.2 us (7%)
  blocking collectives  23.9 us (2%)
  between operations  14.2 us (1%)
    reduce_scatter x2, waiting for transfers between devices, sum_in_order(): pieces = lax.psum_scatter(pieces, axes[k], scatter_dimension=0, tiled=True)  769 us
    dot_general x3, matrix products, deposit(): jnp.einsum('gpy,cgpx->gycx', down_weights, spread, precision=lax.Precisio...  238 us
    scatter-add x3, other arithmetic, one_round(): return tile_sums.at[ids_now].add(deposit_out)  102 us
    dot_general x3, local copies, waits for them, and re-layouts, deposit(): jnp.einsum('gpy,cgpx->gycx', down_weights, spread, precision=lax.Precisio...  39.9 us
  transfers between devices with their start and end apart: 2, of which 2 were waited for; matrix products, arithmetic and copies ran while one was open for 0% of the time, Pallas kernels for 0%

commit v1 on v0

v1 whole, which is shorter than its diff:
```python
import jax
import jax.numpy as jnp
from jax import lax
from jax.experimental import pallas as pl
from jax.experimental.pallas import tpu as pltpu
from jax.sharding import Mesh
from jax.sharding import PartitionSpec as P

TS = 32
FOOT = 16
TILE_DEV = 4
SCREEN = ("screen_0", "screen_1")
DEPTH_SCREEN = ("depth", "screen_0", "screen_1")


def sum_in_order(pieces, axes, turns):
    inside = pieces.shape[1:]
    pieces = pieces.reshape(*(lax.axis_size(a) for a in axes), *inside)
    pieces = jnp.moveaxis(pieces, turns, range(len(axes))).reshape(-1, *inside)
    for k in turns:
        pieces = lax.psum_scatter(pieces, axes[k], scatter_dimension=0, tiled=True)
    return pieces[0]


def cut_along(shard, dim, devices):
    before, after = (shard.shape[:dim], shard.shape[dim + 1 :])
    return jnp.moveaxis(shard.reshape(*before, devices, -1, *after), dim, 0)


def summed_rows(shard, axes, turns, dim):
    devices = lax.axis_size(axes)
    return sum_in_order(cut_along(shard, dim, devices), axes, turns)


BLK = 128
UNR = 32

def deposit_kernel(tile_ref, count_ref, corner_ref, offset_ref, radius_ref, emission_ref, extinction_ref, out_ref, pre_ref):
    step = pl.program_id(0)
    count = count_ref[0, 0]

    @pl.when(step == 0)
    def _():
        def zero(t, c):
            out_ref[t] = jnp.zeros(out_ref.shape[1:], jnp.float32)
            return c
        lax.fori_loop(0, out_ref.shape[0], zero, 0, unroll=8)

    first = step * BLK

    @pl.when(first < count)
    def _():
        slot = first + lax.broadcasted_iota(jnp.int32, (BLK, 128), 0)
        live = slot < count
        radius = radius_ref[0]
        h2 = radius * radius
        h4 = h2 * h2
        scale = jnp.where(live, 1.0 / (h4 * h4), 0.0)
        for k in range(2):
            edge = corner_ref[k, 0].astype(jnp.float32)
            pre_ref[2 * k] = edge
            pre_ref[2 * k + 1] = edge + 16.0 * offset_ref[k, 0] - 0.5
        pre_ref[4] = h2
        for c in range(3):
            pre_ref[5 + c] = emission_ref[c, 0] * scale
        pre_ref[8] = extinction_ref[0] * scale

        rows = lax.broadcasted_iota(jnp.int32, (16, 128), 0).astype(jnp.float32)
        rows16 = rows.astype(jnp.bfloat16)
        zero16 = jnp.zeros((16, 128), jnp.bfloat16)

        def split(w):
            high = w.astype(jnp.bfloat16)
            low = (w - high.astype(jnp.float32)).astype(jnp.bfloat16)
            return high, low

        def one_group(g, c):
            outs = []
            for u in range(UNR):
                j = g * UNR + u
                def row(a):
                    return jnp.broadcast_to(pre_ref[a, pl.ds(j, 1), :], (16, 128))
                h2r = row(4)
                def bump(k):
                    edge = row(2 * k)
                    mask16 = rows16 < edge.astype(jnp.bfloat16)
                    at = jnp.where(rows < edge, rows + 16.0, rows)
                    s = at - row(2 * k + 1)
                    v = jnp.maximum(h2r - s * s, 0.0)
                    return v * v, mask16
                wx, mx = bump(0)
                wy, my = bump(1)
                def spread(w16, m):
                    return [jnp.where(m, zero16, w16), jnp.where(m, w16, zero16)]
                yh, yl = split(wy)
                lhs = jnp.concatenate(spread(yh, my) + spread(yl, my), 0)
                lhs = jnp.concatenate([lhs, lhs], 1)
                hi, lo = [], []
                for ch in range(4):
                    a, b = split(row(5 + ch) * wx)
                    hi += spread(a, mx)
                    lo += spread(b, mx)
                rhs = jnp.concatenate([jnp.concatenate(hi, 0), jnp.concatenate(lo, 0)], 1)
                outs.append(lax.dot_general(lhs, rhs, (((1,), (1,)), ((), ())), preferred_element_type=jnp.float32))
            for u in range(UNR):
                t = tile_ref[0, first + g * UNR + u]
                out_ref[t] += outs[u][:32] + outs[u][32:]
            return c

        groups = lax.div(jnp.minimum(count - first, BLK) + (UNR - 1), UNR)
        lax.fori_loop(0, groups, one_group, 0)


def deposit_all(block_tile, block_count, corner, offset, radius, emission, extinction, tiles=512):
    slots = block_tile.shape[1]
    steps = slots // BLK
    def last(i, tile, count):
        return jnp.minimum(i, lax.div(count[0, 0] - 1, BLK))
    def m4(n):
        return pl.BlockSpec((n, 1, BLK, 128), lambda i, t, c: (0, 0, last(i, t, c), 0))
    def m3():
        return pl.BlockSpec((1, BLK, 128), lambda i, t, c: (0, last(i, t, c), 0))
    return pl.pallas_call(
        deposit_kernel,
        out_shape=jax.ShapeDtypeStruct((tiles, 32, 128), jnp.float32),
        grid_spec=pltpu.PrefetchScalarGridSpec(
            num_scalar_prefetch=2, grid=(steps,),
            in_specs=[m4(2), m4(2), m3(), m4(3), m3()],
            out_specs=pl.BlockSpec((tiles, 32, 128), lambda i, t, c: (0, 0, 0)),
            scratch_shapes=[pltpu.VMEM((9, BLK, 128), jnp.float32)],
        ),
        compiler_params=pltpu.CompilerParams(dimension_semantics=("arbitrary",)),
        name="deposit",
    )(block_tile, block_count, corner, offset, radius, emission, extinction)


def composite(stacked, slab_rank):
    slab_num, tile_num, tile_side, row_width = stacked.shape
    pieces = stacked.reshape(slab_num, tile_num, tile_side, 4, row_width // 4)
    glow_part = pieces[:, :, :, :3, :]
    optical = pieces[:, :, :, 3:, :]
    before = (slab_rank[None, :] < slab_rank[:, None]).astype(jnp.float32)
    prior_depth = jnp.einsum("jk,ktyax->jtyax", before, optical, precision=lax.Precision.HIGHEST)
    lighting = jnp.sum(jnp.exp(-prior_depth) * glow_part * jnp.exp(-0.5 * optical), axis=0)
    coverage = 1.0 - jnp.exp(-jnp.sum(optical, axis=0))
    return jnp.concatenate([lighting, coverage], axis=2).reshape(tile_num, tile_side, row_width)


def shards(block_tile, block_count, slab_rank, corner, offset, radius, emission, extinction):
    depth_size = lax.axis_size("depth")
    screen_size = lax.axis_size(SCREEN)
    partial_value = deposit_all(
        block_tile, block_count, corner, offset, radius, emission, extinction,
        TILE_DEV * depth_size * screen_size,
    )
    shaped = partial_value.reshape(depth_size, screen_size * TILE_DEV, TS, 4 * TS)
    owned = summed_rows(shaped, SCREEN, (1, 0), 1)
    return composite(
        lax.all_to_all(owned, "depth", split_axis=0, concat_axis=0, tiled=True), slab_rank
    )


def solution(mesh):
    torus = Mesh(mesh.devices.reshape(mesh.shape["depth"], 4, 2), ("depth", "screen_0", "screen_1"))
    placed = (
        P("depth", SCREEN),
        P("depth", SCREEN),
        P(),
        P(None, "depth", SCREEN, None),
        P(None, "depth", SCREEN, None),
        P("depth", SCREEN, None),
        P(None, "depth", SCREEN, None),
        P("depth", SCREEN, None),
    )
    return jax.shard_map(
        shards, mesh=torus, in_specs=placed, out_specs=P(DEPTH_SCREEN, None, None), check_vma=False
    )
```

time: 1260 us -> 195 us (0.15)
  waiting for transfers between devices: 769 us -> 107 us
  matrix products: 239 us -> 1.24 us
  other arithmetic: 126 us -> 7.36 us
  local copies, waits for them, and re-layouts: 83.2 us -> 13.1 us
  Pallas kernels: 0 us -> 27.8 us
    reduce_scatter x2, waiting for transfers between devices: 769 us -> 107 us  [sum_in_order(): pieces = lax.psum_scatter(pieces, axes[k], scatter_dimension=0, tiled=True)]
    dot_general x3 -> x0, matrix products: 238 us -> none  [deposit(): jnp.einsum('gpy,cgpx->gycx', down_weights, spread, precision=lax.Precisio...]
    scatter-add x3 -> x0, other arithmetic: 102 us -> none  [one_round(): return tile_sums.at[ids_now].add(deposit_out)]
    dot_general x3 -> x0, local copies, waits for them, and re-layouts: 39.9 us -> none  [deposit(): jnp.einsum('gpy,cgpx->gycx', down_weights, spread, precision=lax.Precisio...]
    pallas_call x0 -> x1, Pallas kernels: none -> 27.8 us  [deposit_all(): pl.pallas_call(deposit_kernel, out_shape=jax.ShapeDtypeStruct((tiles, 32,...]
    reshape x3 -> x0, local copies, waits for them, and re-layouts: 16.5 us -> none  [deposit(): return deposit_out.reshape(deposit_out.shape[0], tile_side, 4 * tile_side)]
where the time goes in v1:
time: 195 us; the launch traced here: 194 us
  waiting for transfers between devices  107 us (55%)
  Pallas kernels  27.8 us (14%)
  blocking collectives  23.9 us (12%)
  between operations  14.1 us (7%)
  local copies, waits for them, and re-layouts  13.1 us (7%)
  other arithmetic  7.36 us (4%)
    reduce_scatter x2, waiting for transfers between devices, sum_in_order(): pieces = lax.psum_scatter(pieces, axes[k], scatter_dimension=0, tiled=True)  107 us
    pallas_call x1, Pallas kernels, deposit_all(): pl.pallas_call(deposit_kernel, out_shape=jax.ShapeDtypeStruct((tiles, 32,...  27.8 us
    all_to_all x1, blocking collectives, shards(): lax.all_to_all(owned, 'depth', split_axis=0, concat_axis=0, tiled=True)  23.9 us
    transpose x1, local copies, waits for them, and re-layouts, sum_in_order(): pieces = jnp.moveaxis(pieces, turns, range(len(axes))).reshape(-1, *inside)  8.47 us
  transfers between devices with their start and end apart: 2, of which 2 were waited for; matrix products, arithmetic and copies ran while one was open for 0% of the time, Pallas kernels for 0%

profile of v1, /device:TPU:0, one launch (start us, length us, event | category | flops | bytes accessed | tf_op | source)
XLA Modules:
  0.0 194.4 jit_solution(11356752415312811791)
XLA Ops:
  6.5 0.0 reduce-scatter.3.cloned.1.call-start
  7.2 27.8 %deposit.1 = f32[512,32,128]{2,1,0:T(8,128)} custom-call(s32[1,2048]{1,0:T(1,128)} %tile_ref.1, s32[1,1]{1,0:T(1,128)S(6)} %copy.26.count_ref, s32[2,1,2048,128]{3,2,1,0:T(8,128)} %corner_ref.1, f32[2,1,2048,128]{3,2,1,0:T(8,128)} %offset_ref.1, f32[1,2048,128]{2,1,0:T(8,128)} %radius_ref.1, f32[3,1,2048,128]{3,2,1,0:T(8,128)} %emission_ref.1, ...), custom_call_target="tpu_custom_call" | custom-call | tf_op jit(solution)/shard_map/deposit/pallas_call | solution.py:123
  35.0 8.5 %copy.13 = f32[2,4,16,4,32,128]{5,4,3,2,1,0:T(8,128)} copy(f32[2,4,16,4,32,128]{5,4,3,0,1,2:T(8,128)} %bitcast.21) | data formatting | bytes 16777216 | tf_op jit(solution)/shard_map/transpose | solution.py:19
  43.4 0.0 reduce-scatter.3.cloned.1.call-update
  43.4 0.0 reduce-scatter.5.cloned.1.call-start
  43.5 56.0 %reduce-scatter.3.cloned.1.call-done = f32[4,16,4,32,128]{4,3,2,1,0:T(8,128)} async-done(((f32[8,16,4,32,128]{4,3,2,1,0:T(8,128)}), f32[4,16,4,32,128]{4,3,2,1,0:T(8,128)}) %reduce-scatter.3.cloned.1.call-update) | async-done | bytes 4194320 | tf_op jit(solution)/shard_map/reduce_scatter | solution.py:21
  99.5 0.0 reduce-scatter.5.cloned.1.call-update
  99.5 50.9 %reduce-scatter.5.cloned.1.call-done = f32[1,16,4,32,128]{4,3,2,1,0:T(8,128)} async-done(((f32[4,16,4,32,128]{4,3,2,1,0:T(8,128)}), f32[1,16,4,32,128]{4,3,2,1,0:T(8,128)}) %reduce-scatter.5.cloned.1.call-update) | async-done | bytes 1048592 | tf_op jit(solution)/shard_map/reduce_scatter | solution.py:21
  150.4 23.9 %all_to_all.5 = f32[16,4,32,128]{3,2,1,0:T(8,128)S(1)} all-to-all(f32[16,4,32,128]{3,2,1,0:T(8,128)} %bitcast.23), channel_id=1, replica_groups=mesh['depth'=16,'screen_0'=4,'screen_1'=2] {'depth'}, dimensions={0} | all-to-all | bytes 2097152 | tf_op jit(solution)/shard_map/all_to_all | solution.py:159
  174.3 0.0 copy-start.1
  174.3 3.1 %reshape.44 = f32[16,4,32,4,32]{4,3,2,1,0:T(4,128)} reshape(f32[16,4,32,128]{3,2,1,0:T(8,128)S(1)} %all_to_all.5) | data formatting | bytes 2097152 | tf_op jit(solution)/shard_map/reshape | solution.py:139
  177.4 3.9 %fusion.9 = (f32[16,4,32,1,32]{4,3,2,1,0:T(1,128)S(1)}, f32[4,32,32]{2,1,0:T(8,128)S(1)}) fusion(f32[16,4,32,4,32]{4,3,2,1,0:T(4,128)} %reshape.44), kind=kLoop, calls=%fused_computation.15 | loop fusion | flops 61440 | bytes 540672 | tf_op jit(solution)/shard_map/slice | solution.py:141
  181.4 0.0 copy-start
  181.4 0.7 exponential_bitcast_fusion
  182.1 0.0 copy-done.1
  182.1 1.2 fusion.2
  183.3 0.3 copy.15
  183.7 0.3 copy.16
  184.0 0.0 copy-done
  184.0 2.6 %fusion.1 = f32[4,32,3,32]{3,2,1,0:T(4,128)S(1)} fusion(f32[16,4,32,4,32]{4,3,2,1,0:T(4,128)S(1)} %copy-done, f32[16,4,32,32]{3,2,1,0:T(8,128)S(1)} %copy.16, f32[16,4,32,32]{3,2,1,0:T(8,128)S(1)} %copy.15), kind=kLoop, calls=%fused_computation.2 | loop fusion | flops 577536 | bytes 1359872 | tf_op jit(solution)/shard_map/reduce_sum | solution.py:144
  186.6 0.1 pad_maximum_fusion
  186.8 0.8 reshape.46
  (1 shorter events, 0.0 us)
Async XLA Ops:
  6.5 93.0 %reduce-scatter.3.cloned.1.call-start = ((), (), s32[]{:S(2)}) async-start(), calls=%async_computation.3 | async-start | bytes 12582912 | tf_op jit(solution)/shard_map/reduce_scatter | solution.py:21
  43.4 107.0 %reduce-scatter.5.cloned.1.call-start = ((), (), s32[]{:S(2)}) async-start(), calls=%async_computation.4 | async-start | bytes 5242880 | tf_op jit(solution)/shard_map/reduce_scatter | solution.py:21
  174.3 7.8 %copy-start.1 = (s32[16]{0:T(128)S(1)}, s32[16]{0:T(128)}, u32[]{:S(2)}) copy-start(s32[16]{0:T(128)} %param.10) | copy-start | bytes 196
  181.4 2.7 %copy-start = (f32[16,4,32,4,32]{4,3,2,1,0:T(4,128)S(1)}, f32[16,4,32,4,32]{4,3,2,1,0:T(4,128)}, u32[]{:S(2)}) copy-start(f32[16,4,32,4,32]{4,3,2,1,0:T(4,128)} %reshape.44) | copy-start | bytes 3145732
Sparse Core Ops, SparseCore 0:
  43.6 55.8 reduce-scatter.2
  101.9 48.4 reduce-scatter.4

commit v2 on v1

--- a/solution.py
+++ b/solution.py
@@ -6,32 +6,8 @@
 from jax.sharding import Mesh
 from jax.sharding import PartitionSpec as P
 
-TS = 32
-FOOT = 16
-TILE_DEV = 4
 SCREEN = ("screen_0", "screen_1")
 DEPTH_SCREEN = ("depth", "screen_0", "screen_1")
-
-
-def sum_in_order(pieces, axes, turns):
-    inside = pieces.shape[1:]
-    pieces = pieces.reshape(*(lax.axis_size(a) for a in axes), *inside)
-    pieces = jnp.moveaxis(pieces, turns, range(len(axes))).reshape(-1, *inside)
-    for k in turns:
-        pieces = lax.psum_scatter(pieces, axes[k], scatter_dimension=0, tiled=True)
-    return pieces[0]
-
-
-def cut_along(shard, dim, devices):
-    before, after = (shard.shape[:dim], shard.shape[dim + 1 :])
-    return jnp.moveaxis(shard.reshape(*before, devices, -1, *after), dim, 0)
-
-
-def summed_rows(shard, axes, turns, dim):
-    devices = lax.axis_size(axes)
-    return sum_in_order(cut_along(shard, dim, devices), axes, turns)
-
-
 BLK = 128
 UNR = 32
 
@@ -134,30 +110,179 @@
     )(block_tile, block_count, corner, offset, radius, emission, extinction)
 
 
-def composite(stacked, slab_rank):
-    slab_num, tile_num, tile_side, row_width = stacked.shape
-    pieces = stacked.reshape(slab_num, tile_num, tile_side, 4, row_width // 4)
-    glow_part = pieces[:, :, :, :3, :]
-    optical = pieces[:, :, :, 3:, :]
-    before = (slab_rank[None, :] < slab_rank[:, None]).astype(jnp.float32)
-    prior_depth = jnp.einsum("jk,ktyax->jtyax", before, optical, precision=lax.Precision.HIGHEST)
-    lighting = jnp.sum(jnp.exp(-prior_depth) * glow_part * jnp.exp(-0.5 * optical), axis=0)
-    coverage = 1.0 - jnp.exp(-jnp.sum(optical, axis=0))
-    return jnp.concatenate([lighting, coverage], axis=2).reshape(tile_num, tile_side, row_width)
+MESH_ID = pl.DeviceIdType.MESH
+
+
+def exchange_kernel(order_ref, partial_ref, image_ref, mine, pair, from_up, from_down, via_up, via_down, stack,
+                    local_sem, pair_send, pair_recv, far_send, far_recv, near_send, near_recv, sum_send, sum_recv,
+                    stack_send, stack_recv):
+    d = lax.axis_index("depth")
+    z = lax.axis_index("screen_0")
+    core = lax.axis_index("screen_1")
+    mate = 1 - core
+    y, x = lax.div(d, 4), lax.rem(d, 4)
+    z_up, z_down, z_far = lax.rem(z + 1, 4), lax.rem(z + 3, 4), lax.rem(z + 2, 4)
+    turns = (2, 1, 3, 0)
+    others = [(ry, rx) for ry in turns for rx in (2, 1, 3, 0) if (ry, rx) != (0, 0)]
+
+    def away(ry, rx):
+        return lax.rem(y + ry, 4) * 4 + lax.rem(x + rx, 4)
+
+    def row(ry):
+        return lax.rem(y + ry, 4) * 4
+
+    barrier = pltpu.get_barrier_semaphore()
+    pl.semaphore_signal(barrier, inc=1, device_id={"screen_1": mate}, device_id_type=MESH_ID)
+    pl.semaphore_signal(barrier, inc=1, device_id={"screen_0": z_up}, device_id_type=MESH_ID)
+    pl.semaphore_signal(barrier, inc=1, device_id={"screen_0": z_down}, device_id_type=MESH_ID)
+    for ry, rx in others:
+        pl.semaphore_signal(barrier, inc=1, device_id={"depth": away(ry, rx)}, device_id_type=MESH_ID)
+
+    places = (z_far, z_up, z_down, z)
+
+    def local_copy(p, g):
+        rows = pl.ds(row(g), 4)
+        return pltpu.make_async_copy(
+            partial_ref.at[rows, places[p], core], mine.at[rows, places[p]], local_sem.at[p, g])
+
+    def pair_copy(p, g):
+        rows = pl.ds(row(g), 4)
+        return pltpu.make_async_remote_copy(
+            partial_ref.at[rows, places[p], mate], pair.at[rows, places[p]],
+            pair_send.at[p, g], pair_recv.at[p, g], device_id={"screen_1": mate}, device_id_type=MESH_ID)
+
+    def line_copy(g, half, place, goal, to_up, send, recv):
+        rows = pl.ds(row(g) + 2 * half, 2)
+        return pltpu.make_async_remote_copy(
+            mine.at[rows, place], goal.at[rows], send.at[to_up, g], recv.at[to_up, g],
+            device_id={"screen_0": z_up if to_up else z_down}, device_id_type=MESH_ID)
+
+    def far_copy(g, to_up):
+        return line_copy(g, 1 - to_up, z_far, via_up if to_up else via_down, to_up, far_send, far_recv)
+
+    def near_copy(g, to_up):
+        return line_copy(g, to_up, z_up if to_up else z_down, from_up if to_up else from_down, to_up,
+                         near_send, near_recv)
+
+    def sum_copy(g, to_up):
+        return line_copy(g, 1 - to_up, z_up if to_up else z_down, from_up if to_up else from_down, to_up,
+                         sum_send, sum_recv)
+
+    def stack_copy(ry, rx):
+        to = away(ry, rx)
+        return pltpu.make_async_remote_copy(
+            mine.at[to, z], stack.at[d], stack_send.at[ry, rx], stack_recv.at[ry, rx],
+            device_id={"depth": to}, device_id_type=MESH_ID)
+
+    def add_in(first, num, place, terms):
+        def one(i, c):
+            total = mine[first + i, place]
+            for term in terms:
+                total = total + term(first + i)
+            mine[first + i, place] = total
+            return c
+        lax.fori_loop(0, num, one, 0)
+
+    for p in range(4):
+        for g in turns:
+            local_copy(p, g).start()
+    pl.semaphore_wait(barrier, 18)
+    for p in range(4):
+        for g in turns:
+            pair_copy(p, g).start()
+
+    def take_pair(p, g):
+        local_copy(p, g).wait()
+        pair_copy(p, g).wait_recv()
+
+    for g in turns:
+        take_pair(0, g)
+        add_in(row(g), 4, z_far, [lambda i: pair[i, z_far]])
+        far_copy(g, 1).start()
+        far_copy(g, 0).start()
+    for g in turns:
+        for p, to_up in ((1, 1), (2, 0)):
+            take_pair(p, g)
+            add_in(row(g), 4, places[p], [lambda i, p=p: pair[i, places[p]]])
+            near_copy(g, to_up).start()
+    for g in turns:
+        for to_up in (1, 0):
+            far_copy(g, to_up).wait_recv()
+            via = via_up if to_up else via_down
+            add_in(row(g) + 2 * (1 - to_up), 2, z_up if to_up else z_down, [lambda i, via=via: via[i]])
+            sum_copy(g, to_up).start()
+    for g in turns:
+        take_pair(3, g)
+        for to_up in (1, 0):
+            near_copy(g, to_up).wait_recv()
+            sum_copy(g, to_up).wait_recv()
+        add_in(row(g), 4, z, [lambda i: pair[i, z], lambda i: from_up[i], lambda i: from_down[i]])
+        for rx in (2, 1, 3, 0):
+            if (g, rx) != (0, 0):
+                stack_copy(g, rx).start()
+    stack[d] = mine[d, z]
+    for ry, rx in others:
+        stack_copy(ry, rx).wait_recv()
+
+    lane = lax.broadcasted_iota(jnp.int32, (32, 128), 1)
+
+    def one_tile(t, c):
+        def one_slab(p, carry):
+            prior, light = carry
+            value = stack[order_ref[p], t]
+            own = jnp.where(lane >= 96, value, 0.0)
+            twice = own + pltpu.roll(own, 32, 1)
+            optical = twice + pltpu.roll(twice, 64, 1)
+            light = light + jnp.exp(-(prior + 0.5 * optical)) * value
+            return prior + optical, light
+        zero = jnp.zeros((32, 128), jnp.float32)
+        prior, light = lax.fori_loop(0, 16, one_slab, (zero, zero), unroll=4)
+        image_ref[t] = jnp.where(lane >= 96, 1.0 - jnp.exp(-prior), light)
+        return c
+    lax.fori_loop(0, 4, one_tile, 0)
+
+    for g in turns:
+        for p in range(4):
+            pair_copy(p, g).wait_send()
+        for to_up in (1, 0):
+            far_copy(g, to_up).wait_send()
+            near_copy(g, to_up).wait_send()
+            sum_copy(g, to_up).wait_send()
+    for ry, rx in others:
+        stack_copy(ry, rx).wait_send()
+
+
+def exchange(partial_value, slab_rank):
+    slots = jnp.arange(16, dtype=jnp.int32)
+    order = jnp.sum(jnp.where(slab_rank[None, :] == slots[:, None], slots[None, :], 0), axis=1)
+    dma = pltpu.SemaphoreType.DMA
+    return pl.pallas_call(
+        exchange_kernel,
+        out_shape=jax.ShapeDtypeStruct((4, 32, 128), jnp.float32),
+        in_specs=[pl.BlockSpec(memory_space=pltpu.SMEM), pl.BlockSpec(memory_space=pl.ANY)],
+        out_specs=pl.BlockSpec(memory_space=pltpu.VMEM),
+        scratch_shapes=[
+            pltpu.VMEM((16, 4, 4, 32, 128), jnp.float32),
+            pltpu.VMEM((16, 4, 4, 32, 128), jnp.float32),
+            pltpu.VMEM((16, 4, 32, 128), jnp.float32),
+            pltpu.VMEM((16, 4, 32, 128), jnp.float32),
+            pltpu.VMEM((16, 4, 32, 128), jnp.float32),
+            pltpu.VMEM((16, 4, 32, 128), jnp.float32),
+            pltpu.VMEM((16, 4, 32, 128), jnp.float32),
+            dma((4, 4)), dma((4, 4)), dma((4, 4)),
+            dma((2, 4)), dma((2, 4)), dma((2, 4)), dma((2, 4)), dma((2, 4)), dma((2, 4)),
+            dma((4, 4)), dma((4, 4)),
+        ],
+        compiler_params=pltpu.CompilerParams(collective_id=0, has_side_effects=True),
+        name="exchange",
+    )(order, partial_value.reshape(16, 4, 2, 4, 32, 128))
 
 
 def shards(block_tile, block_count, slab_rank, corner, offset, radius, emission, extinction):
-    depth_size = lax.axis_size("depth")
-    screen_size = lax.axis_size(SCREEN)
     partial_value = deposit_all(
-        block_tile, block_count, corner, offset, radius, emission, extinction,
-        TILE_DEV * depth_size * screen_size,
+        block_tile, block_count, corner, offset, radius, emission, extinction
     )
-    shaped = partial_value.reshape(depth_size, screen_size * TILE_DEV, TS, 4 * TS)
-    owned = summed_rows(shaped, SCREEN, (1, 0), 1)
-    return composite(
-        lax.all_to_all(owned, "depth", split_axis=0, concat_axis=0, tiled=True), slab_rank
-    )
+    return exchange(partial_value, slab_rank)
 
 
 def solution(mesh):

time: 195 us -> 118 us (0.61)
  waiting for transfers between devices: 107 us -> 0 us
  Pallas kernels: 27.8 us -> 115 us
  blocking collectives: 23.9 us -> 0 us
  between operations: 14.1 us -> 0.66 us
  local copies, waits for them, and re-layouts: 13.1 us -> 1.47 us
  other arithmetic: 7.36 us -> 1.28 us
    reduce_scatter x2 -> x0, waiting for transfers between devices: 107 us -> none  [sum_in_order(): pieces = lax.psum_scatter(pieces, axes[k], scatter_dimension=0, tiled=True)]
    pallas_call x0 -> x1, Pallas kernels: none -> 94 us  [exchange(): pl.pallas_call(exchange_kernel, out_shape=jax.ShapeDtypeStruct((4, 32, 12...]
    all_to_all x1 -> x0, blocking collectives: 23.9 us -> none  [shards(): lax.all_to_all(owned, 'depth', split_axis=0, concat_axis=0, tiled=True)]
    transpose x1 -> x0, local copies, waits for them, and re-layouts: 8.47 us -> none  [sum_in_order(): pieces = jnp.moveaxis(pieces, turns, range(len(axes))).reshape(-1, *inside)]
    pallas_call x1, Pallas kernels: 27.8 us -> 20.8 us  [deposit_all(): pl.pallas_call(deposit_kernel, out_shape=jax.ShapeDtypeStruct((tiles, 32,...]
    reshape x2 -> x0, local copies, waits for them, and re-layouts: 3.93 us -> none  [the longest x1 3.14 us: composite(): pieces = stacked.reshape(slab_num, tile_num, tile_side, 4, row_width // 4)]
    slice x1 -> x0, other arithmetic: 3.89 us -> none  [composite(): optical = pieces[:, :, :, 3:, :]]
  transfers between devices with their start and end apart: 2 -> 0, of which waited for: 2 -> 0; matrix products, arithmetic and copies ran while one was open for 0% -> 0% of each run, Pallas kernels for 0% -> 0%
where the time goes in v2:
time: 118 us
  Pallas kernels  115 us (97%)
  local copies, waits for them, and re-layouts  1.47 us (1%)
  other arithmetic  1.28 us (1%)
    pallas_call x1, Pallas kernels, exchange(): pl.pallas_call(exchange_kernel, out_shape=jax.ShapeDtypeStruct((4, 32, 12...  94 us
    pallas_call x1, Pallas kernels, deposit_all(): pl.pallas_call(deposit_kernel, out_shape=jax.ShapeDtypeStruct((tiles, 32,...  20.8 us

profile of v2, /device:TPU:0, one launch (start us, length us, event | category | flops | bytes accessed | tf_op | source)
XLA Modules:
  0.0 118.2 jit_solution(5507539059254584354)
XLA Ops:
  0.7 1.3 %select_reduce_fusion.order_ref = s32[16]{0:T(128)} fusion(s32[16]{0:T(128)} %param.10), kind=kLoop, calls=%fused_computation | loop fusion | flops 752 | bytes 128 | tf_op jit(solution)/shard_map/reduce_sum | solution.py:257
  1.9 20.8 %deposit.1 = f32[512,32,128]{2,1,0:T(8,128)} custom-call(s32[1,2048]{1,0:T(1,128)} %tile_ref.1, s32[1,1]{1,0:T(1,128)S(6)} %copy.10.count_ref, s32[2,1,2048,128]{3,2,1,0:T(8,128)} %corner_ref.1, f32[2,1,2048,128]{3,2,1,0:T(8,128)} %offset_ref.1, f32[1,2048,128]{2,1,0:T(8,128)} %radius_ref.1, f32[3,1,2048,128]{3,2,1,0:T(8,128)} %emission_ref.1, ...), custom_call_target="tpu_custom_call" | custom-call | tf_op jit(solution)/shard_map/deposit/pallas_call | solution.py:99
  22.7 94.0 %exchange.1 = f32[4,32,128]{2,1,0:T(8,128)} custom-call(s32[16]{0:T(128)} %select_reduce_fusion.order_ref, f32[16,4,2,4,32,128]{5,4,3,2,1,0:T(8,128)} %bitcast.1), custom_call_target="tpu_custom_call" | custom-call | tf_op jit(solution)/shard_map/exchange/pallas_call | solution.py:259
  116.7 1.5 %copy.11 = f32[4,32,128]{2,1,0:T(8,128)} copy(f32[4,32,128]{2,1,0:T(8,128)} %exchange.1) | data formatting | bytes 131072

commit v3 on v2

--- a/solution.py
+++ b/solution.py
@@ -8,8 +8,8 @@
 
 SCREEN = ("screen_0", "screen_1")
 DEPTH_SCREEN = ("depth", "screen_0", "screen_1")
-BLK = 128
-UNR = 32
+BLK = 256
+UNR = 64
 
 def deposit_kernel(tile_ref, count_ref, corner_ref, offset_ref, radius_ref, emission_ref, extinction_ref, out_ref, pre_ref):
     step = pl.program_id(0)
@@ -113,7 +113,7 @@
 MESH_ID = pl.DeviceIdType.MESH
 
 
-def exchange_kernel(order_ref, partial_ref, image_ref, mine, pair, from_up, from_down, via_up, via_down, stack,
+def exchange_kernel(rank_ref, partial_ref, image_ref, order_ref, mine, pair, from_up, from_down, via_up, via_down, stack,
                     local_sem, pair_send, pair_recv, far_send, far_recv, near_send, near_recv, sum_send, sum_recv,
                     stack_send, stack_recv):
     d = lax.axis_index("depth")
@@ -190,6 +190,12 @@
     for p in range(4):
         for g in turns:
             pair_copy(p, g).start()
+
+    for p in range(16):
+        slab = 0
+        for j in range(1, 16):
+            slab = jnp.where(rank_ref[j] == p, j, slab)
+        order_ref[p] = slab
 
     def take_pair(p, g):
         local_copy(p, g).wait()
@@ -253,8 +259,6 @@
 
 
 def exchange(partial_value, slab_rank):
-    slots = jnp.arange(16, dtype=jnp.int32)
-    order = jnp.sum(jnp.where(slab_rank[None, :] == slots[:, None], slots[None, :], 0), axis=1)
     dma = pltpu.SemaphoreType.DMA
     return pl.pallas_call(
         exchange_kernel,
@@ -262,6 +266,7 @@
         in_specs=[pl.BlockSpec(memory_space=pltpu.SMEM), pl.BlockSpec(memory_space=pl.ANY)],
         out_specs=pl.BlockSpec(memory_space=pltpu.VMEM),
         scratch_shapes=[
+            pltpu.SMEM((16,), jnp.int32),
             pltpu.VMEM((16, 4, 4, 32, 128), jnp.float32),
             pltpu.VMEM((16, 4, 4, 32, 128), jnp.float32),
             pltpu.VMEM((16, 4, 32, 128), jnp.float32),
@@ -275,7 +280,7 @@
         ],
         compiler_params=pltpu.CompilerParams(collective_id=0, has_side_effects=True),
         name="exchange",
-    )(order, partial_value.reshape(16, 4, 2, 4, 32, 128))
+    )(slab_rank, partial_value.reshape(16, 4, 2, 4, 32, 128))
 
 
 def shards(block_tile, block_count, slab_rank, corner, offset, radius, emission, extinction):

time: 118 us -> 113 us (0.958)
  the two profiles are of different devices: /device:TPU:0 before, /device:TPU:33 now
where the time goes in v3:
time: 113 us; the launch traced here: 114 us
  Pallas kernels  111 us (98%)
  local copies, waits for them, and re-layouts  1.47 us (1%)
    pallas_call x1, Pallas kernels, exchange(): pl.pallas_call(exchange_kernel, out_shape=jax.ShapeDtypeStruct((4, 32, 12...  91.7 us
    pallas_call x1, Pallas kernels, deposit_all(): pl.pallas_call(deposit_kernel, out_shape=jax.ShapeDtypeStruct((tiles, 32,...  19.7 us

profile of v3, /device:TPU:33, one launch (start us, length us, event | category | flops | bytes accessed | tf_op | source)
XLA Modules:
  0.0 113.5 jit_solution(355254633154167825)
XLA Ops:
  0.7 19.7 %deposit.1 = f32[512,32,128]{2,1,0:T(8,128)} custom-call(s32[1,2048]{1,0:T(1,128)} %tile_ref.1, s32[1,1]{1,0:T(1,128)S(6)} %copy.10.count_ref, s32[2,1,2048,128]{3,2,1,0:T(8,128)} %corner_ref.1, f32[2,1,2048,128]{3,2,1,0:T(8,128)} %offset_ref.1, f32[1,2048,128]{2,1,0:T(8,128)} %radius_ref.1, f32[3,1,2048,128]{3,2,1,0:T(8,128)} %emission_ref.1, ...), custom_call_target="tpu_custom_call" | custom-call | tf_op jit(solution)/shard_map/deposit/pallas_call | solution.py:99
  20.4 91.7 %exchange.1 = f32[4,32,128]{2,1,0:T(8,128)} custom-call(s32[16]{0:T(128)} %rank_ref.1, f32[16,4,2,4,32,128]{5,4,3,2,1,0:T(8,128)} %bitcast.1), custom_call_target="tpu_custom_call" | custom-call | tf_op jit(solution)/shard_map/exchange/pallas_call | solution.py:263
  112.1 1.5 %copy.11 = f32[4,32,128]{2,1,0:T(8,128)} copy(f32[4,32,128]{2,1,0:T(8,128)} %exchange.1) | data formatting | bytes 131072

commit v4 on v3

--- a/solution.py
+++ b/solution.py
@@ -1,3 +1,5 @@
+import functools
+
 import jax
 import jax.numpy as jnp
 from jax import lax
@@ -11,9 +13,72 @@
 BLK = 256
 UNR = 64
 
-def deposit_kernel(tile_ref, count_ref, corner_ref, offset_ref, radius_ref, emission_ref, extinction_ref, out_ref, pre_ref):
+KEPT = 1536
+MESH_ID = pl.DeviceIdType.MESH
+
+
+def share_kernel(tile_ref, count_ref, corner_ref, offset_ref, radius_ref, emission_ref, extinction_ref,
+                 tile_out, count_out, corner_out, offset_out, radius_out, emission_out, extinction_out,
+                 send_sem, recv_sem):
+    mate = 1 - lax.axis_index("screen_1")
+    barrier = pltpu.get_barrier_semaphore()
+    pl.semaphore_signal(barrier, inc=1, device_id={"screen_1": mate}, device_id_type=MESH_ID)
+    pl.semaphore_wait(barrier, 1)
+    given = pl.ds(KEPT, tile_ref.shape[1] - KEPT)
+    pairs = [
+        (tile_ref.at[:, given], tile_out),
+        (count_ref, count_out),
+        (corner_ref.at[0, :, given], corner_out.at[0]),
+        (corner_ref.at[1, :, given], corner_out.at[1]),
+        (offset_ref.at[0, :, given], offset_out.at[0]),
+        (offset_ref.at[1, :, given], offset_out.at[1]),
+        (radius_ref.at[:, given], radius_out),
+        (emission_ref.at[0, :, given], emission_out.at[0]),
+        (emission_ref.at[1, :, given], emission_out.at[1]),
+        (emission_ref.at[2, :, given], emission_out.at[2]),
+        (extinction_ref.at[:, given], extinction_out),
+    ]
+    copies = [
+        pltpu.make_async_remote_copy(
+            source, goal, send_sem.at[n], recv_sem.at[n], device_id={"screen_1": mate}, device_id_type=MESH_ID)
+        for n, (source, goal) in enumerate(pairs)
+    ]
+    for copy in copies:
+        copy.start()
+    for copy in copies:
+        copy.wait()
+
+
+def share(block_tile, block_count, corner, offset, radius, emission, extinction):
+    num = block_tile.shape[1] - KEPT
+    any_spec = pl.BlockSpec(memory_space=pl.ANY)
+    def cut(n, dtype):
+        return jax.ShapeDtypeStruct((n, 1, num, 128), dtype)
+    flat = jax.ShapeDtypeStruct((1, num, 128), jnp.float32)
+    return pl.pallas_call(
+        share_kernel,
+        out_shape=[
+            jax.ShapeDtypeStruct((1, num), jnp.int32),
+            jax.ShapeDtypeStruct(block_count.shape, jnp.int32),
+            cut(2, jnp.int32), cut(2, jnp.float32), flat, cut(3, jnp.float32), flat,
+        ],
+        in_specs=[any_spec] * 7,
+        out_specs=[any_spec] * 7,
+        scratch_shapes=[pltpu.SemaphoreType.DMA((11,)), pltpu.SemaphoreType.DMA((11,))],
+        compiler_params=pltpu.CompilerParams(collective_id=1, has_side_effects=True),
+        name="share",
+    )(block_tile, block_count, corner, offset, radius, emission, extinction)
+
+
+def deposit_kernel(own_steps, tile_ref, count_ref, mate_tile_ref, mate_count_ref, *refs):
+    own_refs, mate_refs, (out_ref, pre_ref) = refs[:5], refs[5:10], refs[10:]
     step = pl.program_id(0)
-    count = count_ref[0, 0]
+    own = step < own_steps
+    first = jnp.minimum(step, own_steps - 1) * BLK
+    mate_first = jnp.maximum(step - own_steps, 0) * BLK
+    own_live = jnp.minimum(count_ref[0, 0], own_steps * BLK) - first
+    mate_live = mate_count_ref[0, 0] - own_steps * BLK - mate_first
+    live_num = jnp.where(own, own_live, mate_live)
 
     @pl.when(step == 0)
     def _():
@@ -22,12 +87,8 @@
             return c
         lax.fori_loop(0, out_ref.shape[0], zero, 0, unroll=8)
 
-    first = step * BLK
-
-    @pl.when(first < count)
-    def _():
-        slot = first + lax.broadcasted_iota(jnp.int32, (BLK, 128), 0)
-        live = slot < count
+    def prepare(corner_ref, offset_ref, radius_ref, emission_ref, extinction_ref):
+        live = lax.broadcasted_iota(jnp.int32, (BLK, 128), 0) < live_num
         radius = radius_ref[0]
         h2 = radius * radius
         h4 = h2 * h2
@@ -41,6 +102,16 @@
             pre_ref[5 + c] = emission_ref[c, 0] * scale
         pre_ref[8] = extinction_ref[0] * scale
 
+    @pl.when(jnp.logical_and(own, live_num > 0))
+    def _():
+        prepare(*own_refs)
+
+    @pl.when(jnp.logical_and(jnp.logical_not(own), live_num > 0))
+    def _():
+        prepare(*mate_refs)
+
+    @pl.when(live_num > 0)
+    def _():
         rows = lax.broadcasted_iota(jnp.int32, (16, 128), 0).astype(jnp.float32)
         rows16 = rows.astype(jnp.bfloat16)
         zero16 = jnp.zeros((16, 128), jnp.bfloat16)
@@ -79,38 +150,40 @@
                 rhs = jnp.concatenate([jnp.concatenate(hi, 0), jnp.concatenate(lo, 0)], 1)
                 outs.append(lax.dot_general(lhs, rhs, (((1,), (1,)), ((), ())), preferred_element_type=jnp.float32))
             for u in range(UNR):
-                t = tile_ref[0, first + g * UNR + u]
+                t = jnp.where(own, tile_ref[0, first + g * UNR + u], mate_tile_ref[0, mate_first + g * UNR + u])
                 out_ref[t] += outs[u][:32] + outs[u][32:]
             return c
 
-        groups = lax.div(jnp.minimum(count - first, BLK) + (UNR - 1), UNR)
+        groups = lax.div(jnp.minimum(live_num, BLK) + (UNR - 1), UNR)
         lax.fori_loop(0, groups, one_group, 0)
 
 
 def deposit_all(block_tile, block_count, corner, offset, radius, emission, extinction, tiles=512):
-    slots = block_tile.shape[1]
-    steps = slots // BLK
-    def last(i, tile, count):
-        return jnp.minimum(i, lax.div(count[0, 0] - 1, BLK))
-    def m4(n):
-        return pl.BlockSpec((n, 1, BLK, 128), lambda i, t, c: (0, 0, last(i, t, c), 0))
-    def m3():
-        return pl.BlockSpec((1, BLK, 128), lambda i, t, c: (0, last(i, t, c), 0))
+    mate_tile, mate_count, *mate_rest = share(block_tile, block_count, corner, offset, radius, emission, extinction)
+    own_steps = KEPT // BLK
+    steps = block_tile.shape[1] // BLK
+    def own_at(i, tile, count, *unused):
+        return jnp.minimum(jnp.minimum(i, own_steps - 1), lax.div(count[0, 0] - 1, BLK))
+    def mate_at(i, *unused):
+        return jnp.maximum(i - own_steps, 0)
+    def specs(at):
+        def m4(n):
+            return pl.BlockSpec((n, 1, BLK, 128), lambda i, *scalars: (0, 0, at(i, *scalars), 0))
+        def m3():
+            return pl.BlockSpec((1, BLK, 128), lambda i, *scalars: (0, at(i, *scalars), 0))
+        return [m4(2), m4(2), m3(), m4(3), m3()]
     return pl.pallas_call(
-        deposit_kernel,
+        functools.partial(deposit_kernel, own_steps),
         out_shape=jax.ShapeDtypeStruct((tiles, 32, 128), jnp.float32),
         grid_spec=pltpu.PrefetchScalarGridSpec(
-            num_scalar_prefetch=2, grid=(steps,),
-            in_specs=[m4(2), m4(2), m3(), m4(3), m3()],
-            out_specs=pl.BlockSpec((tiles, 32, 128), lambda i, t, c: (0, 0, 0)),
+            num_scalar_prefetch=4, grid=(steps,),
+            in_specs=specs(own_at) + specs(mate_at),
+            out_specs=pl.BlockSpec((tiles, 32, 128), lambda i, *scalars: (0, 0, 0)),
             scratch_shapes=[pltpu.VMEM((9, BLK, 128), jnp.float32)],
         ),
         compiler_params=pltpu.CompilerParams(dimension_semantics=("arbitrary",)),
         name="deposit",
-    )(block_tile, block_count, corner, offset, radius, emission, extinction)
-
-
-MESH_ID = pl.DeviceIdType.MESH
+    )(block_tile, block_count, mate_tile, mate_count, corner, offset, radius, emission, extinction, *mate_rest)
 
 
 def exchange_kernel(rank_ref, partial_ref, image_ref, order_ref, mine, pair, from_up, from_down, via_up, via_down, stack,

time: 113 us -> 105 us (0.929)
  the two profiles are of different devices: /device:TPU:33 before, /device:TPU:0 now
where the time goes in v4:
time: 105 us; the launch traced here: 104 us
  Pallas kernels  102 us (97%)
  local copies, waits for them, and re-layouts  1.47 us (1%)
    pallas_call x1, Pallas kernels, exchange(): pl.pallas_call(exchange_kernel, out_shape=jax.ShapeDtypeStruct((4, 32, 12...  67.8 us
    pallas_call x1, Pallas kernels, deposit_all(): pl.pallas_call(functools.partial(deposit_kernel, own_steps), out_shape=ja...  28.7 us
    pallas_call x1, Pallas kernels, share(): pl.pallas_call(share_kernel, out_shape=[jax.ShapeDtypeStruct((1, num), jn...  5.17 us

profile of v4, /device:TPU:0, one launch (start us, length us, event | category | flops | bytes accessed | tf_op | source)
XLA Modules:
  0.0 103.8 jit_solution(82695033838430698)
XLA Ops:
  0.7 5.2 %share.1 = (s32[1,512]{1,0:T(1,128)}, s32[1,1]{1,0:T(1,128)}, s32[2,1,512,128]{3,2,1,0:T(8,128)}, f32[2,1,512,128]{3,2,1,0:T(8,128)}, f32[1,512,128]{2,1,0:T(8,1...) custom-call(s32[1,2048]{1,0:T(1,128)} %tile_ref.3, s32[1,1]{1,0:T(1,128)S(6)} %copy.10.count_ref, ...), custom_call_target="tpu_custom_call" | custom-call | tf_op jit(solution)/shard_map/share/pallas_call | solution.py:58
  5.8 28.7 %deposit.1 = f32[512,32,128]{2,1,0:T(8,128)} custom-call(s32[1,2048]{1,0:T(1,128)} %tile_ref.3, s32[1,1]{1,0:T(1,128)S(6)} %copy.10.count_ref, s32[1,512]{1,0:T(1,128)} %get-tuple-element.12.mate_tile_ref, s32[1,1]{1,0:T(1,128)} %get-tuple-element.13.mate_count_ref, s32[2,1,2048,128]{3,2,1,0:T(8,128)} %refs_0_.1, f32[2,1,2048,128]{3,2,1,0:T(8,128)} %refs_1_.1, ...), custom_call_target="tpu_custom_call" | custom-call | tf_op jit(solution)/shard_map/deposit/pallas_call | solution.py:175
  34.5 67.8 %exchange.1 = f32[4,32,128]{2,1,0:T(8,128)} custom-call(s32[16]{0:T(128)} %rank_ref.1, f32[16,4,2,4,32,128]{5,4,3,2,1,0:T(8,128)} %bitcast.1), custom_call_target="tpu_custom_call" | custom-call | tf_op jit(solution)/shard_map/exchange/pallas_call | solution.py:336
  102.3 1.5 %copy.11 = f32[4,32,128]{2,1,0:T(8,128)} copy(f32[4,32,128]{2,1,0:T(8,128)} %exchange.1) | data formatting | bytes 131072
